TPU v7x, 32 devices: a whole 2x2x4 slice. The times are simulated.
32 devices in a mesh: grp: 2 (over x), slc: 16 (over z, y, core).
Axes of the slice: x: 2, y: 2, z: 4, core: 2. Of those that a mesh axis runs over, the one named last changes fastest.
Arguments:
- stem_tensor: bfloat16 [1024, 1024], P('slc'), may hold values from -6 to 6
- branches: bfloat16 [16, 6, 2, 1024, 1024], P('slc'), may hold values from -0.1875 to 0.1875
- chain_order: int32 [6], replicated, may hold values from 0 to 5, each once
- index_map: int32 [6], replicated, may hold values from 0 to 5, each once
- bitstrings: int32 [128, 16], P('grp'), parts along dimension 0, may hold values from 0 to 1023
- slice_labels: int32 [32], P(('grp', 'slc')), parts along dimension 0, may hold values from 0 to 63, as said below
Outputs:
- amplitudes: float32 [2048, 1024], P(('grp', 'slc')), parts along dimension 0
There are 2 independent parts, one for each index of `grp`. A program takes and returns all parts, laid end to end along the dimension named above; an argument that names none is the same for every part. Nothing has to cross between parts.
Inputs may be any that keep to these rules, and one draw needn't show every extreme that they name: `slice_labels`: the 16 labels are distinct. `index_map`: each step names a different bit. `chain_order`: each branch tensor is contracted once.
All inputs are finite; a program needn't handle non-finite values.
Results may differ from a plain program's by a relative error of at most 0.025.
Values may be sent and summed in bfloat16 or wider, within the bound.
No kernel may reach another device: no remote copies, remote signals or barrier semaphores. Data moves between devices by JAX's collectives and lax.ppermute only.
A program may use at most 128 MiB of HBM per device.

v0:
```python
import jax
import jax.numpy as jnp
from jax import lax
from jax.sharding import PartitionSpec as P


def slice_partial(selected, slot_branches, chain_order, index_map, slice_label):
    current = selected
    product = None
    steps_total = slot_branches.shape[0]
    for step_index in range(steps_total):
        which_bit = jnp.right_shift(slice_label, index_map[step_index]) & 1
        tensor_pick = slot_branches[chain_order[step_index], which_bit]
        product = jnp.dot(current, tensor_pick, preferred_element_type=jnp.float32)
        if step_index < steps_total - 1:
            current = product.astype(jnp.bfloat16)
    return product


def all_slots(rows_part, branches, chain_order, index_map, slice_labels):
    accumulated = slice_partial(rows_part, branches[0], chain_order, index_map, slice_labels[0])
    return accumulated


def per_device(stem_tensor, branches, chain_order, index_map, bitstrings, slice_labels):
    flat_index = bitstrings.reshape(-1)
    initial_rows = jnp.zeros((flat_index.shape[0], stem_tensor.shape[1]), jnp.bfloat16)
    shard_rows = lax.all_gather(stem_tensor, "slc", axis=0, tiled=True)
    inside = (flat_index >= 0) & (flat_index < shard_rows.shape[0])
    picked = jnp.take(shard_rows, jnp.clip(flat_index, 0, shard_rows.shape[0] - 1), axis=0)
    selected = jnp.where(inside[:, None], picked, initial_rows)
    normalizer = float(slice_labels.shape[0] * lax.axis_size("slc")) ** (-0.5)
    accumulated = all_slots(selected, branches, chain_order, index_map, slice_labels)
    result = (
        lax.psum_scatter(
            accumulated.astype(jnp.bfloat16), "slc", scatter_dimension=0, tiled=True
        ).astype(jnp.float32)
        * normalizer
    )
    return result


def solution(mesh):
    placed = (
        P("slc", None),
        P("slc", None, None, None, None),
        P(),
        P(),
        P("grp", None),
        P(("grp", "slc")),
    )
    return jax.shard_map(
        per_device, mesh=mesh, in_specs=placed, out_specs=P(("grp", "slc"), None), check_vma=False
    )
```

profile of v0, /device:TPU:0, one launch (start us, length us, event | category | flops | bytes accessed | tf_op | source)
XLA Modules:
  0.0 153.4 jit_solution(15890043034381603028)
XLA Ops:
  6.5 0.0 all-gather.2.cloned.1.call-start
  6.5 0.7 all-gather.2.cloned.1.call-update
  7.3 0.0 reduce-scatter.2.cloned.1.call-start
  7.3 1.5 %fusion.71 = (s32[1]{0:T(128)}, s32[1]{0:T(128)}, s32[1]{0:T(128)}, s32[1]{0:T(128)}, s32[1]{0:T(128)}, /*index=5*/s32[1]{0:T(128)}) fusion(s32[6]{0:T(128)} %param.8), kind=kLoop, calls=%fused_computation.44 | loop fusion | bytes 48 | tf_op jit(solution)/shard_map/slice | solution.py:13
  17.1 1.5 %fusion.70 = (s32[1]{0:T(128)}, s32[1]{0:T(128)}, s32[1]{0:T(128)}, s32[1]{0:T(128)}, s32[1]{0:T(128)}, /*index=5*/s32[1]{0:T(128)}) fusion(s32[6]{0:T(128)} %param.9), kind=kLoop, calls=%fused_computation.43 | loop fusion | bytes 48 | tf_op jit(solution)/shard_map/slice | solution.py:12
  22.4 0.7 broadcast_clamp_fusion
  23.1 0.1 copy.8
  23.2 0.1 min.18
  23.3 0.1 min.16
  23.3 0.7 compare_and_fusion
  24.0 0.1 copy.7
  24.1 0.1 and.54
  28.1 25.7 %all-gather.2.cloned.1.call-done = bf16[1024,1024]{1,0:T(8,128)(2,1)} async-done(((bf16[64,1024]{1,0:T(8,128)(2,1)}), bf16[1024,1024]{1,0:T(8,128)(2,1)}) %all-gather.2.cloned.1.call-update) | async-done | bytes 2097168 | tf_op jit(solution)/shard_map/all_gather | solution.py:28
  53.8 6.8 %gather_fusion = bf16[1024,1024]{1,0:T(8,128)(2,1)S(1)} fusion(bf16[1024,1024]{1,0:T(8,128)(2,1)} %all-gather.2.cloned.1.call-done, s32[1024]{0:T(1024)S(1)} %broadcast_clamp_fusion.1), kind=kCustom, calls=%fused_computation | custom fusion | bytes 4198400 | tf_op jit(solution)/shard_map/jit(_take)/gather | solution.py:30
  60.6 8.2 %fusion.8 = bf16[1024,1024]{1,0:T(8,128)(2,1)} fusion(bf16[1,6,2,1024,1024]{4,3,2,1,0:T(8,128)(2,1)} %param.7, s32[]{:T(128)S(6)} %select_n.66, s32[]{:T(128)S(6)} %select_n.67, s32[]{:T(128)S(6)} %select_n.64, s32[]{:T(128)S(6)} %select_n.65, bf16[1024,1024]{1,0:T(8,128)(2,1)S(1)} %gather_fusion, pred[1024]{0:T(1024)(128)(4,1)S(1)} %compare_and_fusion.1, ...), kind=kOutput, calls=%fused_computation.9 | convolution fusion | flops 4298113024 | bytes 8390672 | tf_op jit(solution)/shard_map/dot_general | solution.py:14
  68.8 7.3 %fusion.4 = bf16[1024,1024]{1,0:T(8,128)(2,1)S(1)} fusion(bf16[1,6,2,1024,1024]{4,3,2,1,0:T(8,128)(2,1)} %param.7, s32[]{:T(128)S(6)} %select_n.70, s32[]{:T(128)S(6)} %select_n.71, s32[]{:T(128)S(6)} %select_n.68, s32[]{:T(128)S(6)} %select_n.69, bf16[1024,1024]{1,0:T(8,128)(2,1)} %fusion.8), kind=kOutput, calls=%fused_computation.5 | convolution fusion | flops 4296015872 | bytes 8388624 | tf_op jit(solution)/shard_map/dot_general | solution.py:14
  76.2 8.1 %fusion.27 = bf16[1024,1024]{1,0:T(8,128)(2,1)} fusion(bf16[1,6,2,1024,1024]{4,3,2,1,0:T(8,128)(2,1)} %param.7, s32[]{:T(128)S(6)} %select_n.74, s32[]{:T(128)S(6)} %select_n.75, s32[]{:T(128)S(6)} %select_n.72, s32[]{:T(128)S(6)} %select_n.73, bf16[1024,1024]{1,0:T(8,128)(2,1)S(1)} %fusion.4), kind=kOutput, calls=%fused_computation.28 | convolution fusion | flops 4297064448 | bytes 8388624 | tf_op jit(solution)/shard_map/dot_general | solution.py:14
  84.2 0.0 reduce-scatter.2.cloned.1.call-update
  84.3 60.7 %reduce-scatter.2.cloned.1.call-done = bf16[64,1024]{1,0:T(8,128)(2,1)} async-done(((bf16[1024,1024]{1,0:T(8,128)(2,1)}), bf16[64,1024]{1,0:T(8,128)(2,1)}) %reduce-scatter.2.cloned.1.call-update) | async-done | bytes 131088 | tf_op jit(solution)/shard_map/reduce_scatter | solution.py:35
  145.0 1.6 %convert_multiply_fusion = f32[64,1024]{1,0:T(8,128)} fusion(bf16[64,1024]{1,0:T(8,128)(2,1)} %reduce-scatter.2.cloned.1.call-done), kind=kLoop, calls=%fused_computation.31 | loop fusion | flops 131072 | bytes 393216 | tf_op jit(solution)/shard_map/mul | solution.py:35
  (3 shorter events, 0.0 us)
Async XLA Ops:
  6.5 47.2 %all-gather.2.cloned.1.call-start = ((), (), s32[]{:S(2)}) async-start(), calls=%async_computation.1 | async-start | bytes 2228224 | tf_op jit(solution)/shard_map/all_gather | solution.py:28
  7.3 137.7 %reduce-scatter.2.cloned.1.call-start = ((), (), s32[]{:S(2)}) async-start(), calls=%async_computation.2 | async-start | bytes 2228224 | tf_op jit(solution)/shard_map/reduce_scatter | solution.py:35
Sparse Core Ops, SparseCore 0:
  9.5 44.2 all-gather.1
  84.4 60.5 reduce-scatter.1
where the time goes:
time: 154 us; the launch traced here: 153 us
  waiting for transfers between devices  87.1 us (57%)
  between operations  29.3 us (19%)
  matrix products  23.6 us (15%)
  local copies, waits for them, and re-layouts  10.4 us (7%)
  other arithmetic  3.05 us (2%)
    reduce_scatter x1, waiting for transfers between devices, per_device(): lax.psum_scatter(accumulated.astype(jnp.bfloat16), 'slc', scatter_dimensi...  60.7 us
    all_gather x1, waiting for transfers between devices, per_device(): shard_rows = lax.all_gather(stem_tensor, 'slc', axis=0, tiled=True)  25.7 us
    dot_general x3, matrix products, slice_partial(): product = jnp.dot(current, tensor_pick, preferred_element_type=jnp.float32)  23.6 us
    gather x1, local copies, waits for them, and re-layouts, per_device(): jnp.take(shard_rows, jnp.clip(flat_index, 0, shard_rows.shape[0] - 1), ax...  6.84 us
  transfers between devices with their start and end apart: 2, of which 2 were waited for; matrix products, arithmetic and copies ran while one was open for 3% of the time, Pallas kernels for 0%

commit v1 on v0

v1 whole, which is shorter than its diff:
```python
import functools

import jax
import jax.numpy as jnp
from jax import lax
from jax.experimental import pallas as pl
from jax.experimental.pallas import tpu as pltpu
from jax.sharding import PartitionSpec as P


def swap(array, mask, size):
    return lax.ppermute(array, "slc", [(i, i ^ mask) for i in range(size)])


def pick(flag, first, second):
    return jnp.where(flag == 0, first, second)


def chain_body(flip, order_ref, map_ref, label_ref, branches_ref, after_ref, away_ref, keep_ref, tail_ref, full_ref, sems):
    slots, steps = branches_ref.shape[:2]
    width = tail_ref.shape[-1]
    me = lax.axis_index("slc")
    column = pl.multiple_of(((jnp.right_shift(me, 1) & 1) ^ flip) * width, width)

    def load(slot, step):
        which = jnp.right_shift(label_ref[slot], map_ref[step]) & 1
        source = branches_ref.at[slot, order_ref[step], which]
        if step == steps - 1:
            return pltpu.make_async_copy(source.at[:, pl.ds(column, width)], tail_ref, sems.at[step])
        return pltpu.make_async_copy(source, full_ref.at[step], sems.at[step])

    total = None
    for slot in range(slots):
        copies = [load(slot, step) for step in range(steps)]
        for copy in reversed(copies):
            copy.start()
        copies[-1].wait()
        current = tail_ref[...]
        for step in reversed(range(steps - 1)):
            copies[step].wait()
            product = jnp.dot(full_ref[step], current, preferred_element_type=jnp.float32)
            current = product.astype(jnp.bfloat16)
        total = product if total is None else total + product
    total = total.astype(jnp.bfloat16)
    left, right = total[:, : width // 2], total[:, width // 2 :]
    first = (me & 1) == 0
    away_ref[...] = jnp.where(first, right, left)
    keep_ref[...] = jnp.where(first, left, right)


def chain_columns(flip, scalars, branches, after):
    steps, bond = branches.shape[1], branches.shape[-1]
    smem = pl.BlockSpec(memory_space=pltpu.SMEM)
    vmem = pl.BlockSpec(memory_space=pltpu.VMEM)
    quarter = jax.ShapeDtypeStruct((bond, bond // 4), jnp.bfloat16)
    return pl.pallas_call(
        functools.partial(chain_body, flip),
        out_shape=(quarter, quarter),
        in_specs=[smem, smem, smem, pl.BlockSpec(memory_space=pl.ANY), pl.BlockSpec(memory_space=pl.ANY)],
        out_specs=(vmem, vmem),
        scratch_shapes=[
            pltpu.VMEM((bond, bond // 2), jnp.bfloat16),
            pltpu.VMEM((steps - 1, bond, bond), jnp.bfloat16),
            pltpu.SemaphoreType.DMA((steps,)),
        ],
        cost_estimate=pl.CostEstimate(
            flops=branches.size * bond // 2, bytes_accessed=branches.size, transcendentals=0
        ),
    )(*scalars, branches, after)


def amplitudes(stem_tensor, branches, chain_order, index_map, bitstrings, slice_labels):
    size = lax.axis_size("slc")
    me = lax.axis_index("slc")
    scalars = (chain_order, index_map, slice_labels)

    pair = jnp.concatenate([stem_tensor, swap(stem_tensor, 2, size)], axis=0)
    near_rows = jnp.concatenate([pair] + [swap(pair, mask, size) for mask in range(4, size, 4)], axis=0)
    gathered = jnp.concatenate([near_rows, swap(near_rows, 1, size)], axis=0)

    away, keep = chain_columns(1, scalars, branches, pair)
    far = (keep.astype(jnp.float32) + swap(away, 1, size).astype(jnp.float32)).astype(jnp.bfloat16)
    away, keep = chain_columns(0, scalars, branches, far)
    far = swap(far, 2, size)
    own = keep.astype(jnp.float32) + swap(away, 1, size).astype(jnp.float32)
    own = (own + far.astype(jnp.float32)).astype(jnp.bfloat16)

    flat = bitstrings.reshape(-1)
    rows = stem_tensor.shape[0]
    owner = (flat // rows) ^ me
    place = (jnp.right_shift(owner, 1) + (owner & 1) * (size // 2)) * rows + flat % rows
    hot = (place[:, None] == lax.broadcasted_iota(jnp.int32, (flat.shape[0], rows * size), 1)).astype(jnp.bfloat16)

    every = jnp.dot(gathered, own, preferred_element_type=jnp.float32).astype(jnp.bfloat16)
    part = jnp.dot(hot, every, preferred_element_type=jnp.float32).astype(jnp.bfloat16)

    groups = size // 4
    mine = jnp.right_shift(me, 2)
    blocks = part.reshape(groups, part.shape[0] // groups, part.shape[1])
    total = lax.dynamic_index_in_dim(blocks, mine, 0, keepdims=False).astype(jnp.float32)
    for mask in range(1, groups):
        sent = lax.dynamic_index_in_dim(blocks, mine ^ mask, 0, keepdims=False)
        total = total + swap(sent, 4 * mask, size).astype(jnp.float32)

    normalizer = float(slice_labels.shape[0] * size) ** (-0.5)
    quarter = me & 3
    kept = total.astype(jnp.bfloat16).reshape(4, total.shape[0] // 4, total.shape[1])
    got = []
    for mask in range(4):
        sent = lax.dynamic_index_in_dim(kept, quarter ^ mask, 0, keepdims=False)
        got.append(swap(sent, mask, size) if mask else sent)
    low, high = quarter & 1, jnp.right_shift(quarter, 1)
    pairs = [(pick(low, got[m], got[m + 1]), pick(low, got[m + 1], got[m])) for m in (0, 2)]
    columns = [pick(high, pairs[0][i], pairs[1][i]) for i in (0, 1)] + [pick(high, pairs[1][i], pairs[0][i]) for i in (0, 1)]
    return jnp.concatenate(columns, axis=1).astype(jnp.float32) * normalizer


def solution(mesh):
    placed = (
        P("slc", None),
        P("slc", None, None, None, None),
        P(),
        P(),
        P("grp", None),
        P(("grp", "slc")),
    )
    return jax.shard_map(amplitudes, mesh=mesh, in_specs=placed, out_specs=P(("grp", "slc"), None), check_vma=False)
```

time: 154 us -> 93 us (0.60)
  waiting for transfers between devices: 87.1 us -> 41.4 us
  between operations: 29.3 us -> 0.76 us
  Pallas kernels: 0 us -> 19.9 us
  matrix products: 23.6 us -> 4.07 us
  starting transfers between devices: 0.04 us -> 19.1 us
  local copies, waits for them, and re-layouts: 10.4 us -> 5.87 us
    reduce_scatter x1 -> x0, waiting for transfers between devices: 60.7 us -> none  [per_device(): lax.psum_scatter(accumulated.astype(jnp.bfloat16), 'slc', scatter_dimensi...]
    ppermute x0 -> x14, waiting for transfers between devices: none -> 41.4 us  [swap(): return lax.ppermute(array, 'slc', [(i, i ^ mask) for i in range(size)])]
    all_gather x1 -> x0, waiting for transfers between devices: 25.7 us -> none  [per_device(): shard_rows = lax.all_gather(stem_tensor, 'slc', axis=0, tiled=True)]
    pallas_call x0 -> x2, Pallas kernels: none -> 19.9 us  [chain_columns(): pl.pallas_call(functools.partial(chain_body, flip), out_shape=(quarter, q...]
    dot_general x3 -> x1, matrix products: 23.6 us -> 4.07 us  [amplitudes(): jnp.dot(hot, every, preferred_element_type=jnp.float32).astype(jnp.bfloat16)]
    ppermute x0 -> x14, starting transfers between devices: none -> 19.1 us  [swap(): return lax.ppermute(array, 'slc', [(i, i ^ mask) for i in range(size)])]
    gather x1 -> x0, local copies, waits for them, and re-layouts: 6.84 us -> none  [per_device(): jnp.take(shard_rows, jnp.clip(flat_index, 0, shard_rows.shape[0] - 1), ax...]
    unnamed x0 -> x15, local copies, waits for them, and re-layouts: none -> 3.93 us
  transfers between devices with their start and end apart: 2 -> 14, of which waited for: 2 -> 7; matrix products, arithmetic and copies ran while one was open for 3% -> 7% of each run, Pallas kernels for 0% -> 21%
where the time goes in v1:
time: 93 us; the launch traced here: 92.8 us
  waiting for transfers between devices  41.4 us (45%)
  Pallas kernels  19.9 us (21%)
  starting transfers between devices  19.1 us (21%)
  local copies, waits for them, and re-layouts  5.87 us (6%)
  matrix products  4.07 us (4%)
  other arithmetic  1.74 us (2%)
    ppermute x14, waiting for transfers between devices, swap(): return lax.ppermute(array, 'slc', [(i, i ^ mask) for i in range(size)])  41.4 us
    pallas_call x2, Pallas kernels, chain_columns(): pl.pallas_call(functools.partial(chain_body, flip), out_shape=(quarter, q...  19.9 us
    ppermute x14, starting transfers between devices, swap(): return lax.ppermute(array, 'slc', [(i, i ^ mask) for i in range(size)])  19.1 us
    dot_general x1, matrix products, amplitudes(): jnp.dot(hot, every, preferred_element_type=jnp.float32).astype(jnp.bfloat16)  4.07 us
    unnamed x15, local copies, waits for them, and re-layouts  3.93 us
  transfers between devices with their start and end apart: 14, of which 7 were waited for; matrix products, arithmetic and copies ran while one was open for 7% of the time, Pallas kernels for 21%

profile of v1, /device:TPU:0, one launch (start us, length us, event | category | flops | bytes accessed | tf_op | source)
XLA Modules:
  0.0 92.8 jit_solution(5663725887433606940)
XLA Ops:
  0.0 3.0 %collective-permute-start = (bf16[64,1024]{1,0:T(8,128)(2,1)}, bf16[64,1024]{1,0:T(8,128)(2,1)S(1)}, u32[]{:S(2)}, u32[]{:S(2)}) collective-permute-start(bf16[64,1024]{1,0:T(8,128)(2,1)} %param.6), channel_id=1, source_target_pairs={{0,2},{1,3},{2,0},{3,1},{4,6},{5,7},{6,4},{7,5},{8,10},{9,11},{10,... | collective-permute-start | bytes 393224 | tf_op jit(solution)/shard_map/ppermute | solution.py:12
  3.6 1.6 %constant_dynamic-update-slice_fusion.6 = (bf16[512,1024]{1,0:T(8,128)(2,1)S(1)}, bf16[128,1024]{1,0:T(8,128)(2,1)S(1)}, bf16[1024,1024]{1,0:T(8,128)(2,1)}) fusion(bf16[64,1024]{1,0:T(8,128)(2,1)} %param.6), kind=kLoop, calls=%fused_computation.32 | loop fusion | bytes 524288
  5.3 1.4 %collective-permute-done = bf16[64,1024]{1,0:T(8,128)(2,1)S(1)} collective-permute-done((bf16[64,1024]{1,0:T(8,128)(2,1)}, bf16[64,1024]{1,0:T(8,128)(2,1)S(1)}, u32[]{:S(2)}, u32[]{:S(2)}) %collective-permute-start) | collective-permute-done | bytes 131104 | tf_op jit(solution)/shard_map/ppermute | solution.py:12
  6.7 0.7 constant_dynamic-update-slice_fusion.5
  7.4 0.0 copy-start.1
  7.4 1.8 %collective-permute-start.1 = (bf16[128,1024]{1,0:T(8,128)(2,1)S(1)}, bf16[128,1024]{1,0:T(8,128)(2,1)S(1)}, u32[]{:S(2)}, u32[]{:S(2)}) collective-permute-start(bf16[128,1024]{1,0:T(8,128)(2,1)S(1)} %get-tuple-element.31.after_ref), channel_id=1, source_target_pairs={{0,4},{1,5},{2,6},{3,7},{4,0},{5,1},{6,2},{7,3},{8,12},{9,13},{10,... | collective-permute-start | bytes 786440 | tf_op jit(solution)/shard_map/ppermute | solution.py:12
  9.2 0.0 copy-done.1
  9.2 9.9 %shard_map.64 = (bf16[1024,256]{1,0:T(8,128)(2,1)}, bf16[1024,256]{1,0:T(8,128)(2,1)}) custom-call(s32[6]{0:T(128)} %order_ref.3, s32[6]{0:T(128)} %map_ref.3, s32[1]{0:T(128)S(6)} %copy.18.label_ref, bf16[1,6,2,1024,1024]{4,3,2,1,0:T(8,128)(2,1)} %branches_ref.3, bf16[128,1024]{1,0:T(8,128)(2,1)} %copy-done.1), custom_call_target="tpu_custom_call" | custom-call | flops 6442450944 | bytes 12582912 | tf_op jit(solution)/shard_map/pallas_call | solution.py:56
  19.1 0.0 copy-start.2
  19.1 0.1 collective-permute-start.5
  19.2 2.7 %collective-permute-start.2 = (bf16[128,1024]{1,0:T(8,128)(2,1)}, bf16[128,1024]{1,0:T(8,128)(2,1)S(1)}, u32[]{:S(2)}, u32[]{:S(2)}) collective-permute-start(bf16[128,1024]{1,0:T(8,128)(2,1)} %copy-done.1), channel_id=1, source_target_pairs={{0,8},{1,9},{2,10},{3,11},{4,12},{5,13},{6,14},{7,15},{8,0},{9,1},... | collective-permute-start | bytes 786440 | tf_op jit(solution)/shard_map/ppermute | solution.py:12
  21.8 0.5 collective-permute-start.3
  22.3 0.0 collective-permute-done.1
  22.3 0.8 constant_dynamic-update-slice_fusion.4
  23.1 17.4 %collective-permute-done.2 = bf16[128,1024]{1,0:T(8,128)(2,1)S(1)} collective-permute-done((bf16[128,1024]{1,0:T(8,128)(2,1)}, bf16[128,1024]{1,0:T(8,128)(2,1)S(1)}, u32[]{:S(2)}, u32[]{:S(2)}) %collective-permute-start.2) | collective-permute-done | bytes 262176 | tf_op jit(solution)/shard_map/ppermute | solution.py:12
  40.5 0.8 constant_dynamic-update-slice_fusion.3
  41.2 0.0 collective-permute-done.3
  41.2 0.8 constant_dynamic-update-slice_fusion.2
  42.0 0.0 collective-permute-start.4
  42.0 0.0 collective-permute-done.5
  42.0 0.0 copy-done.2
  42.0 0.9 add_convert_fusion.1.after_ref
  43.0 0.0 copy-start
  43.0 0.0 copy-start.3
  43.0 10.0 %shard_map.65 = (bf16[1024,256]{1,0:T(8,128)(2,1)}, bf16[1024,256]{1,0:T(8,128)(2,1)}) custom-call(s32[6]{0:T(128)} %order_ref.3, s32[6]{0:T(128)} %map_ref.3, s32[1]{0:T(128)S(6)} %copy.18.label_ref, bf16[1,6,2,1024,1024]{4,3,2,1,0:T(8,128)(2,1)} %branches_ref.3, bf16[1024,256]{1,0:T(8,128)(2,1)} %add_convert_fusion.1.after_ref), custom_call_target="tpu_custom_call" | custom-call | flops 6442450944 | bytes 12582912 | tf_op jit(solution)/shard_map/pallas_call | solution.py:56
  53.0 0.0 copy-start.4
  53.0 0.6 collective-permute-start.6
  53.6 0.0 copy-done
  53.6 1.5 %collective-permute-start.7 = (bf16[1024,256]{1,0:T(8,128)(2,1)S(1)}, bf16[1024,256]{1,0:T(8,128)(2,1)}, u32[]{:S(2)}, u32[]{:S(2)}) collective-permute-start(bf16[1024,256]{1,0:T(8,128)(2,1)S(1)} %copy-done), channel_id=1, source_target_pairs={{0,2},{1,3},{2,0},{3,1},{4,6},{5,7},{6,4},{7,5},{8,10},{9,11},{10,... | collective-permute-start | bytes 1572872 | tf_op jit(solution)/shard_map/ppermute | solution.py:12
  55.1 0.0 copy-done.3
  55.1 0.1 copy.7
  55.2 0.1 reshape.66
  55.3 0.0 collective-permute-done.4
  55.3 1.0 %constant_dynamic-update-slice_fusion.7 = bf16[1024,1024]{1,0:T(8,128)(2,1)} fusion(bf16[1024,1024]{1,0:T(8,128)(2,1)} %get-tuple-element.17, bf16[512,1024]{1,0:T(8,128)(2,1)S(1)} %collective-permute-done.4), kind=kLoop, calls=%fused_computation.33 | loop fusion | bytes 2097152 | tf_op jit(solution)/shard_map/concatenate | solution.py:79
  56.3 0.0 collective-permute-done.6
  56.3 11.3 %collective-permute-done.7 = bf16[1024,256]{1,0:T(8,128)(2,1)} collective-permute-done((bf16[1024,256]{1,0:T(8,128)(2,1)S(1)}, bf16[1024,256]{1,0:T(8,128)(2,1)}, u32[]{:S(2)}, u32[]{:S(2)}) %collective-permute-start.7) | collective-permute-done | bytes 524320 | tf_op jit(solution)/shard_map/ppermute | solution.py:12
  67.6 0.0 copy-done.4
  67.6 4.1 %fusion.2 = bf16[1024,256]{1,0:T(8,128)(2,1)S(1)} fusion(s32[1024]{0:T(1024)S(1)} %fusion.7, bf16[1024,1024]{1,0:T(8,128)(2,1)} %constant_dynamic-update-slice_fusion.7, bf16[1024,256]{1,0:T(8,128)(2,1)} %collective-permute-done.7, bf16[1024,256]{1,0:T(8,128)(2,1)} %collective-permute-done.6, bf16[1024,256]{1,0:T(8,128)(2,1)S(1)} %copy-done.4), kind=kOutput, calls=%fused_computation.3 | convolution fusion | flops 1076887552 | bytes 4198400 | tf_op jit(solution)/shard_map/dot_general | solution.py:95
  71.7 3.1 %collective-permute-start.10 = (bf16[256,256]{1,0:T(8,128)(2,1)S(1)}, bf16[256,256]{1,0:T(8,128)(2,1)S(1)}, u32[]{:S(2)}, u32[]{:S(2)}) collective-permute-start(bf16[256,256]{1,0:T(8,128)(2,1)S(1)} %get-tuple-element.14), channel_id=1, source_target_pairs={{0,12},{1,13},{2,14},{3,15},{4,8},{5,9},{6,10},{7,11},{8,4},{9,5},... | collective-permute-start | bytes 393224 | tf_op jit(solution)/shard_map/ppermute | solution.py:12
  74.8 4.0 %collective-permute-start.8 = (bf16[256,256]{1,0:T(8,128)(2,1)S(1)}, bf16[256,256]{1,0:T(8,128)(2,1)S(1)}, u32[]{:S(2)}, u32[]{:S(2)}) collective-permute-start(bf16[256,256]{1,0:T(8,128)(2,1)S(1)} %get-tuple-element.13), channel_id=1, source_target_pairs={{0,4},{1,5},{2,6},{3,7},{4,0},{5,1},{6,2},{7,3},{8,12},{9,13},{10,... | collective-permute-start | bytes 393224 | tf_op jit(solution)/shard_map/ppermute | solution.py:12
  78.8 0.0 collective-permute-start.9
  78.8 0.0 collective-permute-done.10
  78.8 3.3 %collective-permute-done.8 = bf16[256,256]{1,0:T(8,128)(2,1)S(1)} collective-permute-done((bf16[256,256]{1,0:T(8,128)(2,1)S(1)}, bf16[256,256]{1,0:T(8,128)(2,1)S(1)}, u32[]{:S(2)}, u32[]{:S(2)}) %collective-permute-start.8) | collective-permute-done | bytes 131104 | tf_op jit(solution)/shard_map/ppermute | solution.py:12
  82.0 4.9 %collective-permute-done.9 = bf16[256,256]{1,0:T(8,128)(2,1)S(1)} collective-permute-done((bf16[256,256]{1,0:T(8,128)(2,1)S(1)}, bf16[256,256]{1,0:T(8,128)(2,1)S(1)}, u32[]{:S(2)}, u32[]{:S(2)}) %collective-permute-start.9) | collective-permute-done | bytes 131104 | tf_op jit(solution)/shard_map/ppermute | solution.py:12
  87.0 0.1 fusion.5
  87.1 0.1 collective-permute-start.11
  87.1 1.6 %collective-permute-start.12 = (bf16[64,256]{1,0:T(8,128)(2,1)S(1)}, bf16[64,256]{1,0:T(8,128)(2,1)S(1)}, u32[]{:S(2)}, u32[]{:S(2)}) collective-permute-start(bf16[64,256]{1,0:T(8,128)(2,1)S(1)} %get-tuple-element.28), channel_id=1, source_target_pairs={{0,2},{1,3},{2,0},{3,1},{4,6},{5,7},{6,4},{7,5},{8,10},{9,11},{10,... | collective-permute-start | bytes 98312 | tf_op jit(solution)/shard_map/ppermute | solution.py:12
  88.7 0.3 collective-permute-start.13
  89.0 0.0 collective-permute-done.11
  89.0 2.1 %collective-permute-done.12 = bf16[64,256]{1,0:T(8,128)(2,1)S(1)} collective-permute-done((bf16[64,256]{1,0:T(8,128)(2,1)S(1)}, bf16[64,256]{1,0:T(8,128)(2,1)S(1)}, u32[]{:S(2)}, u32[]{:S(2)}) %collective-permute-start.12) | collective-permute-done | bytes 32800 | tf_op jit(solution)/shard_map/ppermute | solution.py:12
  91.1 1.0 %collective-permute-done.13 = bf16[64,256]{1,0:T(8,128)(2,1)S(1)} collective-permute-done((bf16[64,256]{1,0:T(8,128)(2,1)S(1)}, bf16[64,256]{1,0:T(8,128)(2,1)S(1)}, u32[]{:S(2)}, u32[]{:S(2)}) %collective-permute-start.13) | collective-permute-done | bytes 32800 | tf_op jit(solution)/shard_map/ppermute | solution.py:12
  92.1 0.7 convert_multiply_fusion
  (4 shorter events, 0.1 us)
Async XLA Ops:
  0.0 6.7 %collective-permute-start = (bf16[64,1024]{1,0:T(8,128)(2,1)}, bf16[64,1024]{1,0:T(8,128)(2,1)S(1)}, u32[]{:S(2)}, u32[]{:S(2)}) collective-permute-start(bf16[64,1024]{1,0:T(8,128)(2,1)} %param.6), channel_id=1, source_target_pairs={{0,2},{1,3},{2,0},{3,1},{4,6},{5,7},{6,4},{7,5},{8,10},{9,11},{10,... | collective-permute-start | bytes 393224 | tf_op jit(solution)/shard_map/ppermute | solution.py:12
  7.4 1.8 %copy-start.1 = (bf16[128,1024]{1,0:T(8,128)(2,1)}, bf16[128,1024]{1,0:T(8,128)(2,1)S(1)}, u32[]{:S(2)}) copy-start(bf16[128,1024]{1,0:T(8,128)(2,1)S(1)} %get-tuple-element.31.after_ref) | copy-start | bytes 786436
  7.4 14.9 %collective-permute-start.1 = (bf16[128,1024]{1,0:T(8,128)(2,1)S(1)}, bf16[128,1024]{1,0:T(8,128)(2,1)S(1)}, u32[]{:S(2)}, u32[]{:S(2)}) collective-permute-start(bf16[128,1024]{1,0:T(8,128)(2,1)S(1)} %get-tuple-element.31.after_ref), channel_id=1, source_target_pairs={{0,4},{1,5},{2,6},{3,7},{4,0},{5,1},{6,2},{7,3},{8,12},{9,13},{10,... | collective-permute-start | bytes 786440 | tf_op jit(solution)/shard_map/ppermute | solution.py:12
  19.1 22.9 %copy-start.2 = (bf16[1024,256]{1,0:T(8,128)(2,1)S(1)}, bf16[1024,256]{1,0:T(8,128)(2,1)}, u32[]{:S(2)}) copy-start(bf16[1024,256]{1,0:T(8,128)(2,1)} %get-tuple-element.9) | copy-start | bytes 1572868
  19.1 22.9 %collective-permute-start.5 = (bf16[1024,256]{1,0:T(8,128)(2,1)}, bf16[1024,256]{1,0:T(8,128)(2,1)S(1)}, u32[]{:S(2)}, u32[]{:S(2)}) collective-permute-start(bf16[1024,256]{1,0:T(8,128)(2,1)} %get-tuple-element.10), channel_id=1, source_target_pairs={{0,1},{1,0},{2,3},{3,2},{4,5},{5,4},{6,7},{7,6},{8,9},{9,8},{10,11... | collective-permute-start | bytes 1572872 | tf_op jit(solution)/shard_map/ppermute | solution.py:12
  19.2 21.3 %collective-permute-start.2 = (bf16[128,1024]{1,0:T(8,128)(2,1)}, bf16[128,1024]{1,0:T(8,128)(2,1)S(1)}, u32[]{:S(2)}, u32[]{:S(2)}) collective-permute-start(bf16[128,1024]{1,0:T(8,128)(2,1)} %copy-done.1), channel_id=1, source_target_pairs={{0,8},{1,9},{2,10},{3,11},{4,12},{5,13},{6,14},{7,15},{8,0},{9,1},... | collective-permute-start | bytes 786440 | tf_op jit(solution)/shard_map/ppermute | solution.py:12
  21.8 19.4 %collective-permute-start.3 = (bf16[128,1024]{1,0:T(8,128)(2,1)}, bf16[128,1024]{1,0:T(8,128)(2,1)S(1)}, u32[]{:S(2)}, u32[]{:S(2)}) collective-permute-start(bf16[128,1024]{1,0:T(8,128)(2,1)} %copy-done.1), channel_id=1, source_target_pairs={{0,12},{1,13},{2,14},{3,15},{4,8},{5,9},{6,10},{7,11},{8,4},{9,5},... | collective-permute-start | bytes 786440 | tf_op jit(solution)/shard_map/ppermute | solution.py:12
  42.0 13.2 %collective-permute-start.4 = (bf16[512,1024]{1,0:T(8,128)(2,1)S(1)}, bf16[512,1024]{1,0:T(8,128)(2,1)S(1)}, u32[]{:S(2)}, u32[]{:S(2)}) collective-permute-start(bf16[512,1024]{1,0:T(8,128)(2,1)S(1)} %get-tuple-element.16), channel_id=1, source_target_pairs={{0,1},{1,0},{2,3},{3,2},{4,5},{5,4},{6,7},{7,6},{8,9},{9,8},{10,11... | collective-permute-start | bytes 3145736 | tf_op jit(solution)/shard_map/ppermute | solution.py:12
  43.0 10.6 %copy-start = (bf16[1024,256]{1,0:T(8,128)(2,1)S(1)}, bf16[1024,256]{1,0:T(8,128)(2,1)}, u32[]{:S(2)}) copy-start(bf16[1024,256]{1,0:T(8,128)(2,1)} %add_convert_fusion.1.after_ref) | copy-start | bytes 1572868
  43.0 12.1 %copy-start.3 = (s32[64,16]{0,1:T(8,128)S(1)}, s32[64,16]{0,1:T(8,128)}, u32[]{:S(2)}) copy-start(s32[64,16]{0,1:T(8,128)} %param.10) | copy-start | bytes 12292
  53.0 14.6 %copy-start.4 = (bf16[1024,256]{1,0:T(8,128)(2,1)S(1)}, bf16[1024,256]{1,0:T(8,128)(2,1)}, u32[]{:S(2)}) copy-start(bf16[1024,256]{1,0:T(8,128)(2,1)} %get-tuple-element.11) | copy-start | bytes 1572868
  53.0 3.3 %collective-permute-start.6 = (bf16[1024,256]{1,0:T(8,128)(2,1)}, bf16[1024,256]{1,0:T(8,128)(2,1)}, u32[]{:S(2)}, u32[]{:S(2)}) collective-permute-start(bf16[1024,256]{1,0:T(8,128)(2,1)} %get-tuple-element.12), channel_id=1, source_target_pairs={{0,1},{1,0},{2,3},{3,2},{4,5},{5,4},{6,7},{7,6},{8,9},{9,8},{10,11... | collective-permute-start | bytes 1572872 | tf_op jit(solution)/shard_map/ppermute | solution.py:12
  53.6 14.0 %collective-permute-start.7 = (bf16[1024,256]{1,0:T(8,128)(2,1)S(1)}, bf16[1024,256]{1,0:T(8,128)(2,1)}, u32[]{:S(2)}, u32[]{:S(2)}) collective-permute-start(bf16[1024,256]{1,0:T(8,128)(2,1)S(1)} %copy-done), channel_id=1, source_target_pairs={{0,2},{1,3},{2,0},{3,1},{4,6},{5,7},{6,4},{7,5},{8,10},{9,11},{10,... | collective-permute-start | bytes 1572872 | tf_op jit(solution)/shard_map/ppermute | solution.py:12
  71.7 7.1 %collective-permute-start.10 = (bf16[256,256]{1,0:T(8,128)(2,1)S(1)}, bf16[256,256]{1,0:T(8,128)(2,1)S(1)}, u32[]{:S(2)}, u32[]{:S(2)}) collective-permute-start(bf16[256,256]{1,0:T(8,128)(2,1)S(1)} %get-tuple-element.14), channel_id=1, source_target_pairs={{0,12},{1,13},{2,14},{3,15},{4,8},{5,9},{6,10},{7,11},{8,4},{9,5},... | collective-permute-start | bytes 393224 | tf_op jit(solution)/shard_map/ppermute | solution.py:12
  74.8 7.3 %collective-permute-start.8 = (bf16[256,256]{1,0:T(8,128)(2,1)S(1)}, bf16[256,256]{1,0:T(8,128)(2,1)S(1)}, u32[]{:S(2)}, u32[]{:S(2)}) collective-permute-start(bf16[256,256]{1,0:T(8,128)(2,1)S(1)} %get-tuple-element.13), channel_id=1, source_target_pairs={{0,4},{1,5},{2,6},{3,7},{4,0},{5,1},{6,2},{7,3},{8,12},{9,13},{10,... | collective-permute-start | bytes 393224 | tf_op jit(solution)/shard_map/ppermute | solution.py:12
  78.8 8.2 %collective-permute-start.9 = (bf16[256,256]{1,0:T(8,128)(2,1)S(1)}, bf16[256,256]{1,0:T(8,128)(2,1)S(1)}, u32[]{:S(2)}, u32[]{:S(2)}) collective-permute-start(bf16[256,256]{1,0:T(8,128)(2,1)S(1)} %get-tuple-element.15), channel_id=1, source_target_pairs={{0,8},{1,9},{2,10},{3,11},{4,12},{5,13},{6,14},{7,15},{8,0},{9,1},... | collective-permute-start | bytes 393224 | tf_op jit(solution)/shard_map/ppermute | solution.py:12
  87.1 1.9 %collective-permute-start.11 = (bf16[64,256]{1,0:T(8,128)(2,1)S(1)}, bf16[64,256]{1,0:T(8,128)(2,1)S(1)}, u32[]{:S(2)}, u32[]{:S(2)}) collective-permute-start(bf16[64,256]{1,0:T(8,128)(2,1)S(1)} %get-tuple-element.26), channel_id=1, source_target_pairs={{0,1},{1,0},{2,3},{3,2},{4,5},{5,4},{6,7},{7,6},{8,9},{9,8},{10,11... | collective-permute-start | bytes 98312 | tf_op jit(solution)/shard_map/ppermute | solution.py:12
  87.1 4.0 %collective-permute-start.12 = (bf16[64,256]{1,0:T(8,128)(2,1)S(1)}, bf16[64,256]{1,0:T(8,128)(2,1)S(1)}, u32[]{:S(2)}, u32[]{:S(2)}) collective-permute-start(bf16[64,256]{1,0:T(8,128)(2,1)S(1)} %get-tuple-element.28), channel_id=1, source_target_pairs={{0,2},{1,3},{2,0},{3,1},{4,6},{5,7},{6,4},{7,5},{8,10},{9,11},{10,... | collective-permute-start | bytes 98312 | tf_op jit(solution)/shard_map/ppermute | solution.py:12
  88.7 3.4 %collective-permute-start.13 = (bf16[64,256]{1,0:T(8,128)(2,1)S(1)}, bf16[64,256]{1,0:T(8,128)(2,1)S(1)}, u32[]{:S(2)}, u32[]{:S(2)}) collective-permute-start(bf16[64,256]{1,0:T(8,128)(2,1)S(1)} %get-tuple-element.27), channel_id=1, source_target_pairs={{0,3},{1,2},{2,1},{3,0},{4,7},{5,6},{6,5},{7,4},{8,11},{9,10},{10,... | collective-permute-start | bytes 98312 | tf_op jit(solution)/shard_map/ppermute | solution.py:12
